TPU v7x, 32 devices: a whole 2x2x4 slice. The times are simulated.
32 devices in a mesh: section: 2 (over x), dp: 16 (over z, y, core).
Axes of the slice: x: 2, y: 2, z: 4, core: 2. Of those that a mesh axis runs over, the one named last changes fastest.
Arguments:
- inputs: bfloat16 [2048, 8192], P('dp', 'section'), may hold values from -6 to 6
- cotangent: bfloat16 [2048, 8192], P('dp', 'section'), may hold values from -6 to 6
- weights: bfloat16 [2, 64, 8192], P('section'), may hold values from -0.0625 to 0.0625
- momentum: bfloat16 [2, 16, 64, 8192], P('section', 'dp'), may hold values from -6 to 6
- keep_index: int32 [2, 16, 128, 32], P('section', 'dp'), may hold values from 0 to 4095, as said below
Outputs:
- momentum_out: bfloat16 [2, 16, 64, 8192], P('section', 'dp')
- update: bfloat16 [2, 16, 64, 8192], P('section', 'dp')
Inputs may be any that keep to these rules, and one draw needn't show every extreme that they name: `keep_index`: the 32 positions of one block of one replica and layer are all different.
All inputs are finite; a program needn't handle non-finite values.
Results may differ from a plain program's by a relative error of at most 0.0095.
Values may be sent and summed in bfloat16 or wider, within the bound.
A program may use at most 64 MiB of HBM per device.

v0:
```python
import math
import jax
import jax.numpy as jnp
from jax import lax
from jax.sharding import PartitionSpec as P

MICRO = 8
DECAY = 0.999


def from_behind(value, axis, steps):
    count = lax.axis_size(axis)
    leading, last = (max(0, -steps), min(count, count - steps))
    return lax.ppermute(value, axis, [(source, source + steps) for source in range(leading, last)])


def dct_basis(length):
    freq = jnp.arange(length, dtype=jnp.float32)[:, None]
    position = jnp.arange(length, dtype=jnp.float32)[None, :]
    dct_table = jnp.cos(math.pi * (position + 0.5) * freq / length) * math.sqrt(2.0 / length)
    return jnp.where(freq == 0, dct_table * math.sqrt(0.5), dct_table)


def forward_groups(field_in, dct_table):
    row_count, columns = field_in.shape
    blocks = field_in.reshape(row_count // 64, 64, columns // 64, 64)
    coeffs = jnp.einsum(
        "kn,anbm,jm->akbj", dct_table, blocks, dct_table, precision=lax.Precision.HIGHEST
    )
    return coeffs.reshape(-1)


def inverse_groups(flat_in, dct_table, row_count, columns):
    blocks = flat_in.reshape(row_count // 64, 64, columns // 64, 64)
    field_out = jnp.einsum(
        "kn,akbj,jm->anbm", dct_table, blocks, dct_table, precision=lax.Precision.HIGHEST
    )
    return field_out.reshape(row_count, columns)


def group_offsets(position, col_groups):
    group_id = jnp.arange(position.shape[0], dtype=jnp.int32)[:, None]
    return (
        group_id // col_groups * (4096 * col_groups)
        + position // 64 * (64 * col_groups)
        + group_id % col_groups * 64
        + position % 64
    )


def silu_slope(pre_act):
    sigma_h = jax.nn.sigmoid(pre_act)
    return sigma_h * (1.0 + pre_act * (1.0 - sigma_h))


def store_slot(saved, value, slot_clip, is_valid):
    previous = lax.dynamic_index_in_dim(saved, slot_clip, 0, keepdims=False)
    return lax.dynamic_update_index_in_dim(
        saved, jnp.where(is_valid, value, previous), slot_clip, 0
    )


def local(inputs, cotangent, weights, momentum, keep_index):
    sections = lax.axis_size("section")
    section_index = lax.axis_index("section")
    whole_inputs, whole_grads = (
        lax.all_gather(inputs, "section", axis=1, tiled=True),
        lax.all_gather(cotangent, "section", axis=1, tiled=True),
    )
    weight = weights[0]
    row_count, columns = weight.shape
    tok_dev = whole_inputs.shape[0]
    tok_mb = tok_dev // MICRO
    tick_count = MICRO + sections - 1
    first_in = whole_inputs.reshape(MICRO, tok_mb, columns)
    last_grad = whole_grads.reshape(MICRO, tok_mb, columns)

    def forward_tick(tick_idx, loop_state):
        incoming, saved_x, saved_a, saved_h = loop_state
        micro_slot = tick_idx - section_index
        is_valid = (micro_slot >= 0) & (micro_slot < MICRO)
        slot_clip = jnp.clip(micro_slot, 0, MICRO - 1)
        own_first = lax.dynamic_index_in_dim(first_in, slot_clip, 0, keepdims=False)
        activation = jnp.where(section_index == 0, own_first, incoming)
        pre_act = jnp.einsum("td,cd->tc", activation, weight, preferred_element_type=jnp.float32)
        gated_act = jax.nn.silu(pre_act).astype(jnp.bfloat16)
        result = (
            activation.astype(jnp.float32)
            + jnp.einsum("tc,cd->td", gated_act, weight, preferred_element_type=jnp.float32)
        ).astype(jnp.bfloat16)
        saved_x = store_slot(saved_x, activation, slot_clip, is_valid)
        saved_a = store_slot(saved_a, gated_act, slot_clip, is_valid)
        saved_h = store_slot(saved_h, pre_act, slot_clip, is_valid)
        outgoing = from_behind(result, "section", 1)
        return (outgoing, saved_x, saved_a, saved_h)

    start_state = (
        jnp.zeros((tok_mb, columns), jnp.bfloat16),
        jnp.zeros((MICRO, tok_mb, columns), jnp.bfloat16),
        jnp.zeros((MICRO, tok_mb, row_count), jnp.bfloat16),
        jnp.zeros((MICRO, tok_mb, row_count), jnp.float32),
    )
    loop_state = lax.fori_loop(0, tick_count, forward_tick, start_state)
    saved_x, saved_a, saved_h = (loop_state[1], loop_state[2], loop_state[3])

    def backward_tick(tick_idx, loop_state):
        incoming, saved_g, saved_d = loop_state
        micro_slot = tick_idx - (sections - 1 - section_index)
        is_valid = (micro_slot >= 0) & (micro_slot < MICRO)
        slot_clip = jnp.clip(micro_slot, 0, MICRO - 1)
        own_last = lax.dynamic_index_in_dim(last_grad, slot_clip, 0, keepdims=False)
        grad_in = jnp.where(section_index == sections - 1, own_last, incoming)
        pre_act = lax.dynamic_index_in_dim(saved_h, slot_clip, 0, keepdims=False)
        errors = jnp.einsum("td,cd->tc", grad_in, weight, preferred_element_type=jnp.float32)
        deltas = (errors * silu_slope(pre_act)).astype(jnp.bfloat16)
        saved_g = store_slot(saved_g, grad_in, slot_clip, is_valid)
        saved_d = store_slot(saved_d, deltas, slot_clip, is_valid)
        sent_back = (
            grad_in.astype(jnp.float32)
            + jnp.einsum("tc,cd->td", deltas, weight, preferred_element_type=jnp.float32)
        ).astype(jnp.bfloat16)
        outgoing = from_behind(sent_back, "section", -1)
        return (outgoing, saved_g, saved_d)

    back_state = (
        jnp.zeros((tok_mb, columns), jnp.bfloat16),
        jnp.zeros((MICRO, tok_mb, columns), jnp.bfloat16),
        jnp.zeros((MICRO, tok_mb, row_count), jnp.bfloat16),
    )
    back_out = lax.fori_loop(0, tick_count, backward_tick, back_state)
    saved_g = back_out[1].reshape(tok_dev, columns)
    saved_d = back_out[2].reshape(tok_dev, row_count)
    grad_total = jnp.einsum(
        "tc,td->cd",
        saved_a.reshape(tok_dev, row_count),
        saved_g,
        preferred_element_type=jnp.float32,
    )
    grad_total = grad_total + jnp.einsum(
        "tc,td->cd", saved_d, saved_x.reshape(tok_dev, columns), preferred_element_type=jnp.float32
    )
    dct_table = dct_basis(64)
    momentum_new = DECAY * momentum[0, 0].astype(jnp.float32) + grad_total
    coeffs = forward_groups(momentum_new, dct_table)
    offsets = group_offsets(keep_index[0, 0], columns // 64)
    kept_values = coeffs[offsets]
    own_sparse = jnp.zeros_like(coeffs).at[offsets.reshape(-1)].add(kept_values.reshape(-1))
    own_field = inverse_groups(own_sparse, dct_table, row_count, columns)
    momentum_out = (momentum_new - own_field).astype(jnp.bfloat16)
    update = lax.psum(own_field, "dp")
    return (momentum_out[None, None], update.astype(jnp.bfloat16)[None, None])


def solution(mesh):
    return jax.shard_map(
        local,
        mesh=mesh,
        in_specs=(
            P("dp", "section"),
            P("dp", "section"),
            P("section", None, None),
            P("section", "dp", None, None),
            P("section", "dp", None, None),
        ),
        out_specs=(P("section", "dp", None, None), P("section", "dp", None, None)),
        check_vma=False,
    )
```

profile of v0, /device:TPU:0, one launch (start us, length us, event | category | flops | bytes accessed | tf_op | source)
XLA Modules:
  0.0 467.1 jit_solution(12507494876444105098)
XLA Ops:
  10.7 34.7 %all-gather.3.cloned.1.call-done = bf16[128,8192]{1,0:T(8,128)(2,1)} async-done(((bf16[128,4096]{1,0:T(8,128)(2,1)}), bf16[128,8192]{1,0:T(8,128)(2,1)}) %all-gather.3.cloned.1.call-update) | async-done | bytes 2097168 | tf_op jit(solution)/shard_map/all_gather | solution.py:67
  46.3 116.0 %while.39 = (s32[]{:T(128)}, bf16[16,8192]{1,0:T(8,128)(2,1)}, bf16[8,16,8192]{2,1,0:T(8,128)(2,1)S(1)}, bf16[8,16,64]{2,1,0:T(8,128)(2,1)S(1)}, f32[8,16,64]{2,...) while((s32[]{:T(128)}, bf16[16,8192]{1,0:T(8,128)(2,1)}, ...), condition=%wide.region_1.2_spmd, body=%wide.region_0.1_spmd.sunk | while | flops 34222088 | bytes 6873366 | solution.py:103
  51.3 8.7 %collective-permute-done = bf16[16,8192]{1,0:T(8,128)(2,1)S(1)} collective-permute-done((bf16[16,8192]{1,0:T(8,128)(2,1)}, bf16[16,8192]{1,0:T(8,128)(2,1)S(1)}, u32[]{:S(2)}, u32[]{:S(2)}) %collective-permute-start) | collective-permute-done | bytes 262176 | tf_op jit(solution)/shard_map/while/body/eval_jaxpr/ppermute | solution.py:14
  63.2 4.4 collective-permute-start
  67.6 11.2 %collective-permute-done = bf16[16,8192]{1,0:T(8,128)(2,1)S(1)} collective-permute-done((bf16[16,8192]{1,0:T(8,128)(2,1)}, bf16[16,8192]{1,0:T(8,128)(2,1)S(1)}, u32[]{:S(2)}, u32[]{:S(2)}) %collective-permute-start) | collective-permute-done | bytes 262176 | tf_op jit(solution)/shard_map/while/body/eval_jaxpr/ppermute | solution.py:14
  82.1 4.4 collective-permute-start
  94.0 4.4 collective-permute-start
  105.8 4.4 collective-permute-start
  129.3 4.4 collective-permute-start
  145.4 4.4 collective-permute-done
  165.4 131.1 %while.40 = (s32[]{:T(128)}, bf16[16,8192]{1,0:T(8,128)(2,1)}, bf16[8,16,8192]{2,1,0:T(8,128)(2,1)}, bf16[8,16,64]{2,1,0:T(8,128)(2,1)}, pred[]{:T(512)}, /*inde...) while((s32[]{:T(128)}, bf16[16,8192]{1,0:T(8,128)(2,1)}, ...), condition=%wide.region_3.4_spmd, body=%wide.region_2.3_spmd.sunk | while | flops 34220040 | bytes 6834956 | solution.py:130
  171.4 7.3 %collective-permute-done.1 = bf16[16,8192]{1,0:T(8,128)(2,1)S(1)} collective-permute-done((bf16[16,8192]{1,0:T(8,128)(2,1)S(1)}, bf16[16,8192]{1,0:T(8,128)(2,1)S(1)}, u32[]{:S(2)}, u32[]{:S(2)}) %collective-permute-start.1) | collective-permute-done | bytes 262176 | tf_op jit(solution)/shard_map/while/body/eval_jaxpr/ppermute | solution.py:14
  185.5 8.4 %collective-permute-done.1 = bf16[16,8192]{1,0:T(8,128)(2,1)S(1)} collective-permute-done((bf16[16,8192]{1,0:T(8,128)(2,1)S(1)}, bf16[16,8192]{1,0:T(8,128)(2,1)S(1)}, u32[]{:S(2)}, u32[]{:S(2)}) %collective-permute-start.1) | collective-permute-done | bytes 262176 | tf_op jit(solution)/shard_map/while/body/eval_jaxpr/ppermute | solution.py:14
  200.6 9.6 %collective-permute-done.1 = bf16[16,8192]{1,0:T(8,128)(2,1)S(1)} collective-permute-done((bf16[16,8192]{1,0:T(8,128)(2,1)S(1)}, bf16[16,8192]{1,0:T(8,128)(2,1)S(1)}, u32[]{:S(2)}, u32[]{:S(2)}) %collective-permute-start.1) | collective-permute-done | bytes 262176 | tf_op jit(solution)/shard_map/while/body/eval_jaxpr/ppermute | solution.py:14
  216.9 8.9 %collective-permute-done.1 = bf16[16,8192]{1,0:T(8,128)(2,1)S(1)} collective-permute-done((bf16[16,8192]{1,0:T(8,128)(2,1)S(1)}, bf16[16,8192]{1,0:T(8,128)(2,1)S(1)}, u32[]{:S(2)}, u32[]{:S(2)}) %collective-permute-start.1) | collective-permute-done | bytes 262176 | tf_op jit(solution)/shard_map/while/body/eval_jaxpr/ppermute | solution.py:14
  232.6 8.1 %collective-permute-done.1 = bf16[16,8192]{1,0:T(8,128)(2,1)S(1)} collective-permute-done((bf16[16,8192]{1,0:T(8,128)(2,1)S(1)}, bf16[16,8192]{1,0:T(8,128)(2,1)S(1)}, u32[]{:S(2)}, u32[]{:S(2)}) %collective-permute-start.1) | collective-permute-done | bytes 262176 | tf_op jit(solution)/shard_map/while/body/eval_jaxpr/ppermute | solution.py:14
  247.4 7.2 %collective-permute-done.1 = bf16[16,8192]{1,0:T(8,128)(2,1)S(1)} collective-permute-done((bf16[16,8192]{1,0:T(8,128)(2,1)S(1)}, bf16[16,8192]{1,0:T(8,128)(2,1)S(1)}, u32[]{:S(2)}, u32[]{:S(2)}) %collective-permute-start.1) | collective-permute-done | bytes 262176 | tf_op jit(solution)/shard_map/while/body/eval_jaxpr/ppermute | solution.py:14
  261.3 7.0 %collective-permute-done.1 = bf16[16,8192]{1,0:T(8,128)(2,1)S(1)} collective-permute-done((bf16[16,8192]{1,0:T(8,128)(2,1)S(1)}, bf16[16,8192]{1,0:T(8,128)(2,1)S(1)}, u32[]{:S(2)}, u32[]{:S(2)}) %collective-permute-start.1) | collective-permute-done | bytes 262176 | tf_op jit(solution)/shard_map/while/body/eval_jaxpr/ppermute | solution.py:14
  275.0 7.0 %collective-permute-done.1 = bf16[16,8192]{1,0:T(8,128)(2,1)S(1)} collective-permute-done((bf16[16,8192]{1,0:T(8,128)(2,1)S(1)}, bf16[16,8192]{1,0:T(8,128)(2,1)S(1)}, u32[]{:S(2)}, u32[]{:S(2)}) %collective-permute-start.1) | collective-permute-done | bytes 262176 | tf_op jit(solution)/shard_map/while/body/eval_jaxpr/ppermute | solution.py:14
  288.7 7.0 %collective-permute-done.1 = bf16[16,8192]{1,0:T(8,128)(2,1)S(1)} collective-permute-done((bf16[16,8192]{1,0:T(8,128)(2,1)S(1)}, bf16[16,8192]{1,0:T(8,128)(2,1)S(1)}, u32[]{:S(2)}, u32[]{:S(2)}) %collective-permute-start.1) | collective-permute-done | bytes 262176 | tf_op jit(solution)/shard_map/while/body/eval_jaxpr/ppermute | solution.py:14
  320.3 23.0 %gather_fusion = f32[4096]{0:T(1024)S(1)} fusion(f32[524288]{0:T(1024)S(1)} %reshape.407, s32[4096]{0:T(1024)S(1)} %broadcast_clamp_fusion), kind=kCustom, calls=%fused_computation | custom fusion | bytes 49152 | tf_op jit(solution)/shard_map/gather | solution.py:146
  343.3 22.6 %scatter_custom_fusion = f32[524288]{0:T(1024)S(1)} fusion(s32[4096]{0:T(1024)S(1)} %bitcast.169, f32[4096]{0:T(1024)S(1)} %gather_fusion, f32[]{:T(128)} %constant.209.clone.1), kind=kCustom, calls=%fused_computation.46 | custom fusion | flops 4096 | bytes 2097156 | tf_op jit(solution)/shard_map/scatter-add | solution.py:147
  380.1 5.0 %reshape.410 = f32[64,8192]{1,0:T(8,128)} reshape(f32[1,64,128,64]{3,2,1,0:T(8,128)} %copy.13) | data formatting | bytes 4194304 | tf_op jit(solution)/shard_map/reshape | solution.py:38
  387.9 72.4 %all-reduce.1 = bf16[64,8192]{1,0:T(8,128)(2,1)} all-reduce(f32[64,8192]{1,0:T(8,128)} %reshape.410), channel_id=1, replica_groups=mesh['section'=2,'dp'=16] {'dp'}, use_global_device_ids=true, to_apply=%region_5.6 | all-reduce | flops 524288 | bytes 3145728 | tf_op jit(solution)/shard_map/psum | solution.py:150
  (223 shorter events, 178.1 us)
Async XLA Ops:
  7.2 38.2 %all-gather.3.cloned.1.call-start = ((), (), s32[]{:S(2)}) async-start(), calls=%async_computation | async-start | bytes 3145728 | tf_op jit(solution)/shard_map/all_gather | solution.py:67
  7.9 38.4 %copy-start = (bf16[1,64,8192]{2,1,0:T(8,128)(2,1)S(1)}, bf16[1,64,8192]{2,1,0:T(8,128)(2,1)}, u32[]{:S(2)}) copy-start(bf16[1,64,8192]{2,1,0:T(8,128)(2,1)} %param.11) | copy-start | bytes 3145732
  7.9 154.4 %all-gather.5.cloned.1.call-start = ((), (), s32[]{:S(2)}) async-start(), calls=%async_computation.1 | async-start | bytes 3145728 | tf_op jit(solution)/shard_map/all_gather | solution.py:68
  48.9 11.1 %collective-permute-start = (bf16[16,8192]{1,0:T(8,128)(2,1)}, bf16[16,8192]{1,0:T(8,128)(2,1)S(1)}, u32[]{:S(2)}, u32[]{:S(2)}) collective-permute-start(bf16[16,8192]{1,0:T(8,128)(2,1)} %fusion.98), channel_id=1, source_target_pairs={{0,16},{1,17},{2,18},{3,19},{4,20},{5,21},{6,22},{7,23},{8,24},{9,... | collective-permute-start | bytes 786440 | tf_op jit(solution)/shard_map/while/body/eval_jaxpr/ppermute | solution.py:14
  63.2 15.6 %collective-permute-start = (bf16[16,8192]{1,0:T(8,128)(2,1)}, bf16[16,8192]{1,0:T(8,128)(2,1)S(1)}, u32[]{:S(2)}, u32[]{:S(2)}) collective-permute-start(bf16[16,8192]{1,0:T(8,128)(2,1)} %fusion.98), channel_id=1, source_target_pairs={{0,16},{1,17},{2,18},{3,19},{4,20},{5,21},{6,22},{7,23},{8,24},{9,... | collective-permute-start | bytes 786440 | tf_op jit(solution)/shard_map/while/body/eval_jaxpr/ppermute | solution.py:14
  82.1 8.7 %collective-permute-start = (bf16[16,8192]{1,0:T(8,128)(2,1)}, bf16[16,8192]{1,0:T(8,128)(2,1)S(1)}, u32[]{:S(2)}, u32[]{:S(2)}) collective-permute-start(bf16[16,8192]{1,0:T(8,128)(2,1)} %fusion.98), channel_id=1, source_target_pairs={{0,16},{1,17},{2,18},{3,19},{4,20},{5,21},{6,22},{7,23},{8,24},{9,... | collective-permute-start | bytes 786440 | tf_op jit(solution)/shard_map/while/body/eval_jaxpr/ppermute | solution.py:14
  94.0 8.5 %collective-permute-start = (bf16[16,8192]{1,0:T(8,128)(2,1)}, bf16[16,8192]{1,0:T(8,128)(2,1)S(1)}, u32[]{:S(2)}, u32[]{:S(2)}) collective-permute-start(bf16[16,8192]{1,0:T(8,128)(2,1)} %fusion.98), channel_id=1, source_target_pairs={{0,16},{1,17},{2,18},{3,19},{4,20},{5,21},{6,22},{7,23},{8,24},{9,... | collective-permute-start | bytes 786440 | tf_op jit(solution)/shard_map/while/body/eval_jaxpr/ppermute | solution.py:14
  105.8 8.5 %collective-permute-start = (bf16[16,8192]{1,0:T(8,128)(2,1)}, bf16[16,8192]{1,0:T(8,128)(2,1)S(1)}, u32[]{:S(2)}, u32[]{:S(2)}) collective-permute-start(bf16[16,8192]{1,0:T(8,128)(2,1)} %fusion.98), channel_id=1, source_target_pairs={{0,16},{1,17},{2,18},{3,19},{4,20},{5,21},{6,22},{7,23},{8,24},{9,... | collective-permute-start | bytes 786440 | tf_op jit(solution)/shard_map/while/body/eval_jaxpr/ppermute | solution.py:14
  117.5 8.5 %collective-permute-start = (bf16[16,8192]{1,0:T(8,128)(2,1)}, bf16[16,8192]{1,0:T(8,128)(2,1)S(1)}, u32[]{:S(2)}, u32[]{:S(2)}) collective-permute-start(bf16[16,8192]{1,0:T(8,128)(2,1)} %fusion.98), channel_id=1, source_target_pairs={{0,16},{1,17},{2,18},{3,19},{4,20},{5,21},{6,22},{7,23},{8,24},{9,... | collective-permute-start | bytes 786440 | tf_op jit(solution)/shard_map/while/body/eval_jaxpr/ppermute | solution.py:14
  129.3 8.5 %collective-permute-start = (bf16[16,8192]{1,0:T(8,128)(2,1)}, bf16[16,8192]{1,0:T(8,128)(2,1)S(1)}, u32[]{:S(2)}, u32[]{:S(2)}) collective-permute-start(bf16[16,8192]{1,0:T(8,128)(2,1)} %fusion.98), channel_id=1, source_target_pairs={{0,16},{1,17},{2,18},{3,19},{4,20},{5,21},{6,22},{7,23},{8,24},{9,... | collective-permute-start | bytes 786440 | tf_op jit(solution)/shard_map/while/body/eval_jaxpr/ppermute | solution.py:14
  141.0 8.8 %collective-permute-start = (bf16[16,8192]{1,0:T(8,128)(2,1)}, bf16[16,8192]{1,0:T(8,128)(2,1)S(1)}, u32[]{:S(2)}, u32[]{:S(2)}) collective-permute-start(bf16[16,8192]{1,0:T(8,128)(2,1)} %fusion.98), channel_id=1, source_target_pairs={{0,16},{1,17},{2,18},{3,19},{4,20},{5,21},{6,22},{7,23},{8,24},{9,... | collective-permute-start | bytes 786440 | tf_op jit(solution)/shard_map/while/body/eval_jaxpr/ppermute | solution.py:14
  153.1 8.5 %collective-permute-start = (bf16[16,8192]{1,0:T(8,128)(2,1)}, bf16[16,8192]{1,0:T(8,128)(2,1)S(1)}, u32[]{:S(2)}, u32[]{:S(2)}) collective-permute-start(bf16[16,8192]{1,0:T(8,128)(2,1)} %fusion.98), channel_id=1, source_target_pairs={{0,16},{1,17},{2,18},{3,19},{4,20},{5,21},{6,22},{7,23},{8,24},{9,... | collective-permute-start | bytes 786440 | tf_op jit(solution)/shard_map/while/body/eval_jaxpr/ppermute | solution.py:14
  170.1 8.6 %collective-permute-start.1 = (bf16[16,8192]{1,0:T(8,128)(2,1)S(1)}, bf16[16,8192]{1,0:T(8,128)(2,1)S(1)}, u32[]{:S(2)}, u32[]{:S(2)}) collective-permute-start(bf16[16,8192]{1,0:T(8,128)(2,1)S(1)} %fusion.103), channel_id=1, source_target_pairs={{16,0},{17,1},{18,2},{19,3},{20,4},{21,5},{22,6},{23,7},{24,8},{25... | collective-permute-start | bytes 786440 | tf_op jit(solution)/shard_map/while/body/eval_jaxpr/ppermute | solution.py:14
  184.1 9.7 %collective-permute-start.1 = (bf16[16,8192]{1,0:T(8,128)(2,1)S(1)}, bf16[16,8192]{1,0:T(8,128)(2,1)S(1)}, u32[]{:S(2)}, u32[]{:S(2)}) collective-permute-start(bf16[16,8192]{1,0:T(8,128)(2,1)S(1)} %fusion.103), channel_id=1, source_target_pairs={{16,0},{17,1},{18,2},{19,3},{20,4},{21,5},{22,6},{23,7},{24,8},{25... | collective-permute-start | bytes 786440 | tf_op jit(solution)/shard_map/while/body/eval_jaxpr/ppermute | solution.py:14
  199.3 10.9 %collective-permute-start.1 = (bf16[16,8192]{1,0:T(8,128)(2,1)S(1)}, bf16[16,8192]{1,0:T(8,128)(2,1)S(1)}, u32[]{:S(2)}, u32[]{:S(2)}) collective-permute-start(bf16[16,8192]{1,0:T(8,128)(2,1)S(1)} %fusion.103), channel_id=1, source_target_pairs={{16,0},{17,1},{18,2},{19,3},{20,4},{21,5},{22,6},{23,7},{24,8},{25... | collective-permute-start | bytes 786440 | tf_op jit(solution)/shard_map/while/body/eval_jaxpr/ppermute | solution.py:14
  215.6 10.2 %collective-permute-start.1 = (bf16[16,8192]{1,0:T(8,128)(2,1)S(1)}, bf16[16,8192]{1,0:T(8,128)(2,1)S(1)}, u32[]{:S(2)}, u32[]{:S(2)}) collective-permute-start(bf16[16,8192]{1,0:T(8,128)(2,1)S(1)} %fusion.103), channel_id=1, source_target_pairs={{16,0},{17,1},{18,2},{19,3},{20,4},{21,5},{22,6},{23,7},{24,8},{25... | collective-permute-start | bytes 786440 | tf_op jit(solution)/shard_map/while/body/eval_jaxpr/ppermute | solution.py:14
  231.3 9.4 %collective-permute-start.1 = (bf16[16,8192]{1,0:T(8,128)(2,1)S(1)}, bf16[16,8192]{1,0:T(8,128)(2,1)S(1)}, u32[]{:S(2)}, u32[]{:S(2)}) collective-permute-start(bf16[16,8192]{1,0:T(8,128)(2,1)S(1)} %fusion.103), channel_id=1, source_target_pairs={{16,0},{17,1},{18,2},{19,3},{20,4},{21,5},{22,6},{23,7},{24,8},{25... | collective-permute-start | bytes 786440 | tf_op jit(solution)/shard_map/while/body/eval_jaxpr/ppermute | solution.py:14
  246.1 8.5 %collective-permute-start.1 = (bf16[16,8192]{1,0:T(8,128)(2,1)S(1)}, bf16[16,8192]{1,0:T(8,128)(2,1)S(1)}, u32[]{:S(2)}, u32[]{:S(2)}) collective-permute-start(bf16[16,8192]{1,0:T(8,128)(2,1)S(1)} %fusion.103), channel_id=1, source_target_pairs={{16,0},{17,1},{18,2},{19,3},{20,4},{21,5},{22,6},{23,7},{24,8},{25... | collective-permute-start | bytes 786440 | tf_op jit(solution)/shard_map/while/body/eval_jaxpr/ppermute | solution.py:14
  260.0 8.3 %collective-permute-start.1 = (bf16[16,8192]{1,0:T(8,128)(2,1)S(1)}, bf16[16,8192]{1,0:T(8,128)(2,1)S(1)}, u32[]{:S(2)}, u32[]{:S(2)}) collective-permute-start(bf16[16,8192]{1,0:T(8,128)(2,1)S(1)} %fusion.103), channel_id=1, source_target_pairs={{16,0},{17,1},{18,2},{19,3},{20,4},{21,5},{22,6},{23,7},{24,8},{25... | collective-permute-start | bytes 786440 | tf_op jit(solution)/shard_map/while/body/eval_jaxpr/ppermute | solution.py:14
  273.7 8.3 %collective-permute-start.1 = (bf16[16,8192]{1,0:T(8,128)(2,1)S(1)}, bf16[16,8192]{1,0:T(8,128)(2,1)S(1)}, u32[]{:S(2)}, u32[]{:S(2)}) collective-permute-start(bf16[16,8192]{1,0:T(8,128)(2,1)S(1)} %fusion.103), channel_id=1, source_target_pairs={{16,0},{17,1},{18,2},{19,3},{20,4},{21,5},{22,6},{23,7},{24,8},{25... | collective-permute-start | bytes 786440 | tf_op jit(solution)/shard_map/while/body/eval_jaxpr/ppermute | solution.py:14
  287.4 8.3 %collective-permute-start.1 = (bf16[16,8192]{1,0:T(8,128)(2,1)S(1)}, bf16[16,8192]{1,0:T(8,128)(2,1)S(1)}, u32[]{:S(2)}, u32[]{:S(2)}) collective-permute-start(bf16[16,8192]{1,0:T(8,128)(2,1)S(1)} %fusion.103), channel_id=1, source_target_pairs={{16,0},{17,1},{18,2},{19,3},{20,4},{21,5},{22,6},{23,7},{24,8},{25... | collective-permute-start | bytes 786440 | tf_op jit(solution)/shard_map/while/body/eval_jaxpr/ppermute | solution.py:14
  302.8 4.2 copy-start.10
  302.8 4.2 copy-start.11
  380.1 5.0 %copy-start.2 = (f32[64,8192]{1,0:T(8,128)S(1)}, f32[64,8192]{1,0:T(8,128)}, u32[]{:S(2)}) copy-start(f32[64,8192]{1,0:T(8,128)} %copy-done.1) | copy-start | bytes 6291460
  (24 other events, 28.5 us)
Sparse Core Ops, SparseCore 0:
  9.5 35.8 all-gather.2
  46.9 39.2 all-gather.4
where the time goes:
time: 469 us; the launch traced here: 467 us
  waiting for transfers between devices  156 us (33%)
  local copies, waits for them, and re-layouts  82.7 us (18%)
  blocking collectives  72.4 us (15%)
  other arithmetic  52.9 us (11%)
  starting transfers between devices  48.9 us (10%)
  matrix products  39.7 us (8%)
  between operations  14.2 us (3%)
    ppermute x18, waiting for transfers between devices, from_behind(): lax.ppermute(value, axis, [(source, source + steps) for source in range(l...  120 us
    psum x1, blocking collectives, local(): update = lax.psum(own_field, 'dp')  72.4 us
    ppermute x18, starting transfers between devices, from_behind(): lax.ppermute(value, axis, [(source, source + steps) for source in range(l...  48.8 us
    all_gather x1, waiting for transfers between devices, local(): lax.all_gather(inputs, 'section', axis=1, tiled=True)  34.7 us
    dynamic_update_slice x27, other arithmetic, store_slot(): lax.dynamic_update_index_in_dim(saved, jnp.where(is_valid, value, previou...  26.2 us
    gather x1, local copies, waits for them, and re-layouts, local(): kept_values = coeffs[offsets]  23 us
    scatter-add x1, other arithmetic, local(): jnp.zeros_like(coeffs).at[offsets.reshape(-1)].add(kept_values.reshape(-1))  22.6 us
    dynamic_slice x45, local copies, waits for them, and re-layouts, store_slot(): previous = lax.dynamic_index_in_dim(saved, slot_clip, 0, keepdims=False)  15.3 us
  transfers between devices with their start and end apart: 20, of which 19 were waited for; matrix products, arithmetic and copies ran while one was open for 5% of the time, Pallas kernels for 0%

commit v1 on v0

--- a/solution.py
+++ b/solution.py
@@ -6,6 +6,11 @@
 
 MICRO = 8
 DECAY = 0.999
+
+
+def add_all(x, mesh_axis):
+    parts = lax.all_gather(x, mesh_axis)
+    return jnp.sum(parts, axis=0)
 
 
 def from_behind(value, axis, steps):
@@ -147,7 +152,7 @@
     own_sparse = jnp.zeros_like(coeffs).at[offsets.reshape(-1)].add(kept_values.reshape(-1))
     own_field = inverse_groups(own_sparse, dct_table, row_count, columns)
     momentum_out = (momentum_new - own_field).astype(jnp.bfloat16)
-    update = lax.psum(own_field, "dp")
+    update = add_all(own_field, "dp")
     return (momentum_out[None, None], update.astype(jnp.bfloat16)[None, None])
 
 

time: 469 us -> 601 us (1.28)
  waiting for transfers between devices: 156 us -> 342 us
  blocking collectives: 72.4 us -> 0 us
  other arithmetic: 52.9 us -> 65.7 us
    all_gather x0 -> x1, waiting for transfers between devices: none -> 160 us  [add_all(): parts = lax.all_gather(x, mesh_axis)]
    psum x1 -> x0, blocking collectives: 72.4 us -> none  [local(): update = lax.psum(own_field, 'dp')]
    all_gather x1, waiting for transfers between devices: 0.01 us -> 34.7 us  [local(): lax.all_gather(cotangent, 'section', axis=1, tiled=True)]
    reduce_sum x0 -> x1, other arithmetic: none -> 12.8 us  [add_all(): return jnp.sum(parts, axis=0)]
    ppermute x18, waiting for transfers between devices: 120 us -> 111 us  [from_behind(): lax.ppermute(value, axis, [(source, source + steps) for source in range(l...]
    another operation x8 -> x9, local copies, waits for them, and re-layouts: 9.8 us -> 14.5 us
  transfers between devices with their start and end apart: 20 -> 21, of which waited for: 19 -> 21; matrix products, arithmetic and copies ran while one was open for 5% -> 2% of each run, Pallas kernels for 0% -> 0%
where the time goes in v1:
time: 601 us; the launch traced here: 599 us
  waiting for transfers between devices  342 us (57%)
  local copies, waits for them, and re-layouts  87.3 us (15%)
  other arithmetic  65.7 us (11%)
  starting transfers between devices  49 us (8%)
  matrix products  40.4 us (7%)
  between operations  13.9 us (2%)
    all_gather x1, waiting for transfers between devices, add_all(): parts = lax.all_gather(x, mesh_axis)  160 us
    ppermute x18, waiting for transfers between devices, from_behind(): lax.ppermute(value, axis, [(source, source + steps) for source in range(l...  111 us
    ppermute x18, starting transfers between devices, from_behind(): lax.ppermute(value, axis, [(source, source + steps) for source in range(l...  48.8 us
    all_gather x1, waiting for transfers between devices, local(): lax.all_gather(cotangent, 'section', axis=1, tiled=True)  34.7 us
    all_gather x1, waiting for transfers between devices, local(): lax.all_gather(inputs, 'section', axis=1, tiled=True)  34.6 us
    dynamic_update_slice x27, other arithmetic, store_slot(): lax.dynamic_update_index_in_dim(saved, jnp.where(is_valid, value, previou...  26.3 us
    gather x1, local copies, waits for them, and re-layouts, local(): kept_values = coeffs[offsets]  23 us
    scatter-add x1, other arithmetic, local(): jnp.zeros_like(coeffs).at[offsets.reshape(-1)].add(kept_values.reshape(-1))  22.6 us
  transfers between devices with their start and end apart: 21, of which 21 were waited for; matrix products, arithmetic and copies ran while one was open for 2% of the time, Pallas kernels for 0%

profile of v1, /device:TPU:0, one launch (start us, length us, event | category | flops | bytes accessed | tf_op | source)
XLA Modules:
  0.0 598.9 jit_solution(10184977070354423985)
XLA Ops:
  10.8 34.6 %all-gather.4.cloned.1.call-done = bf16[128,8192]{1,0:T(8,128)(2,1)} async-done(((bf16[128,4096]{1,0:T(8,128)(2,1)}), bf16[128,8192]{1,0:T(8,128)(2,1)}) %all-gather.4.cloned.1.call-update) | async-done | bytes 2097168 | tf_op jit(solution)/shard_map/all_gather | solution.py:72
  45.4 34.7 %all-gather.6.cloned.1.call-done = bf16[128,8192]{1,0:T(8,128)(2,1)} async-done(((bf16[128,4096]{1,0:T(8,128)(2,1)}), bf16[128,8192]{1,0:T(8,128)(2,1)}) %all-gather.6.cloned.1.call-update) | async-done | bytes 2097168 | tf_op jit(solution)/shard_map/all_gather | solution.py:73
  81.0 107.0 %while.39 = (s32[]{:T(128)}, bf16[16,8192]{1,0:T(8,128)(2,1)}, bf16[8,16,8192]{2,1,0:T(8,128)(2,1)S(1)}, bf16[8,16,64]{2,1,0:T(8,128)(2,1)S(1)}, f32[8,16,64]{2,...) while((s32[]{:T(128)}, bf16[16,8192]{1,0:T(8,128)(2,1)}, ...), condition=%wide.region_1.2_spmd, body=%wide.region_0.1_spmd.sunk | while | flops 34222088 | bytes 6873366 | solution.py:108
  85.9 5.8 collective-permute-done
  95.0 4.4 collective-permute-start
  99.4 5.0 collective-permute-done
  107.5 4.4 collective-permute-start
  170.6 4.9 collective-permute-done
  191.0 131.2 %while.40 = (s32[]{:T(128)}, bf16[16,8192]{1,0:T(8,128)(2,1)}, bf16[8,16,8192]{2,1,0:T(8,128)(2,1)}, bf16[8,16,64]{2,1,0:T(8,128)(2,1)}, pred[]{:T(512)}, /*inde...) while((s32[]{:T(128)}, bf16[16,8192]{1,0:T(8,128)(2,1)}, ...), condition=%wide.region_3.4_spmd, body=%wide.region_2.3_spmd.sunk | while | flops 34220040 | bytes 6834956 | solution.py:135
  197.0 7.7 %collective-permute-done.1 = bf16[16,8192]{1,0:T(8,128)(2,1)S(1)} collective-permute-done((bf16[16,8192]{1,0:T(8,128)(2,1)S(1)}, bf16[16,8192]{1,0:T(8,128)(2,1)S(1)}, u32[]{:S(2)}, u32[]{:S(2)}) %collective-permute-start.1) | collective-permute-done | bytes 262176 | tf_op jit(solution)/shard_map/while/body/eval_jaxpr/ppermute | solution.py:19
  211.5 8.9 %collective-permute-done.1 = bf16[16,8192]{1,0:T(8,128)(2,1)S(1)} collective-permute-done((bf16[16,8192]{1,0:T(8,128)(2,1)S(1)}, bf16[16,8192]{1,0:T(8,128)(2,1)S(1)}, u32[]{:S(2)}, u32[]{:S(2)}) %collective-permute-start.1) | collective-permute-done | bytes 262176 | tf_op jit(solution)/shard_map/while/body/eval_jaxpr/ppermute | solution.py:19
  227.2 9.5 %collective-permute-done.1 = bf16[16,8192]{1,0:T(8,128)(2,1)S(1)} collective-permute-done((bf16[16,8192]{1,0:T(8,128)(2,1)S(1)}, bf16[16,8192]{1,0:T(8,128)(2,1)S(1)}, u32[]{:S(2)}, u32[]{:S(2)}) %collective-permute-start.1) | collective-permute-done | bytes 262176 | tf_op jit(solution)/shard_map/while/body/eval_jaxpr/ppermute | solution.py:19
  243.5 8.6 %collective-permute-done.1 = bf16[16,8192]{1,0:T(8,128)(2,1)S(1)} collective-permute-done((bf16[16,8192]{1,0:T(8,128)(2,1)S(1)}, bf16[16,8192]{1,0:T(8,128)(2,1)S(1)}, u32[]{:S(2)}, u32[]{:S(2)}) %collective-permute-start.1) | collective-permute-done | bytes 262176 | tf_op jit(solution)/shard_map/while/body/eval_jaxpr/ppermute | solution.py:19
  258.9 7.8 %collective-permute-done.1 = bf16[16,8192]{1,0:T(8,128)(2,1)S(1)} collective-permute-done((bf16[16,8192]{1,0:T(8,128)(2,1)S(1)}, bf16[16,8192]{1,0:T(8,128)(2,1)S(1)}, u32[]{:S(2)}, u32[]{:S(2)}) %collective-permute-start.1) | collective-permute-done | bytes 262176 | tf_op jit(solution)/shard_map/while/body/eval_jaxpr/ppermute | solution.py:19
  273.4 7.0 %collective-permute-done.1 = bf16[16,8192]{1,0:T(8,128)(2,1)S(1)} collective-permute-done((bf16[16,8192]{1,0:T(8,128)(2,1)S(1)}, bf16[16,8192]{1,0:T(8,128)(2,1)S(1)}, u32[]{:S(2)}, u32[]{:S(2)}) %collective-permute-start.1) | collective-permute-done | bytes 262176 | tf_op jit(solution)/shard_map/while/body/eval_jaxpr/ppermute | solution.py:19
  287.1 7.0 %collective-permute-done.1 = bf16[16,8192]{1,0:T(8,128)(2,1)S(1)} collective-permute-done((bf16[16,8192]{1,0:T(8,128)(2,1)S(1)}, bf16[16,8192]{1,0:T(8,128)(2,1)S(1)}, u32[]{:S(2)}, u32[]{:S(2)}) %collective-permute-start.1) | collective-permute-done | bytes 262176 | tf_op jit(solution)/shard_map/while/body/eval_jaxpr/ppermute | solution.py:19
  300.8 7.0 %collective-permute-done.1 = bf16[16,8192]{1,0:T(8,128)(2,1)S(1)} collective-permute-done((bf16[16,8192]{1,0:T(8,128)(2,1)S(1)}, bf16[16,8192]{1,0:T(8,128)(2,1)S(1)}, u32[]{:S(2)}, u32[]{:S(2)}) %collective-permute-start.1) | collective-permute-done | bytes 262176 | tf_op jit(solution)/shard_map/while/body/eval_jaxpr/ppermute | solution.py:19
  314.5 7.0 %collective-permute-done.1 = bf16[16,8192]{1,0:T(8,128)(2,1)S(1)} collective-permute-done((bf16[16,8192]{1,0:T(8,128)(2,1)S(1)}, bf16[16,8192]{1,0:T(8,128)(2,1)S(1)}, u32[]{:S(2)}, u32[]{:S(2)}) %collective-permute-start.1) | collective-permute-done | bytes 262176 | tf_op jit(solution)/shard_map/while/body/eval_jaxpr/ppermute | solution.py:19
  346.7 23.0 %gather_fusion = f32[4096]{0:T(1024)S(1)} fusion(f32[524288]{0:T(1024)S(1)} %reshape.415, s32[4096]{0:T(1024)S(1)} %broadcast_clamp_fusion), kind=kCustom, calls=%fused_computation | custom fusion | bytes 49152 | tf_op jit(solution)/shard_map/gather | solution.py:151
  369.8 22.6 %scatter_custom_fusion = f32[524288]{0:T(1024)S(1)} fusion(s32[4096]{0:T(1024)S(1)} %bitcast.172, f32[4096]{0:T(1024)S(1)} %gather_fusion, f32[]{:T(128)} %constant.210.clone.1), kind=kCustom, calls=%fused_computation.46 | custom fusion | flops 4096 | bytes 2097156 | tf_op jit(solution)/shard_map/scatter-add | solution.py:152
  406.7 4.8 all_gather_reshape.3
  411.6 4.9 reshape.418
  419.2 160.4 %all-gather.8.cloned.1.call-done = f32[16,64,8192]{2,1,0:T(8,128)} async-done(((f32[1,64,8192]{2,1,0:T(8,128)}), f32[16,64,8192]{2,1,0:T(8,128)}) %all-gather.8.cloned.1.call-update) | async-done | bytes 33554448 | tf_op jit(solution)/shard_map/all_gather | solution.py:12
  579.6 12.8 %reduce_sum.9 = bf16[64,8192]{1,0:T(8,128)(2,1)} reduce(f32[16,64,8192]{2,1,0:T(8,128)} %all-gather.8.cloned.1.call-done, f32[]{:T(128)} %constant.210.clone.1), dimensions={0}, to_apply=%region_5.6 | reduce | flops 7864320 | bytes 34603012 | tf_op jit(solution)/shard_map/reduce_sum | solution.py:13
  (225 shorter events, 191.8 us)
Async XLA Ops:
  7.2 38.2 %all-gather.4.cloned.1.call-start = ((), (), s32[]{:S(2)}) async-start(), calls=%async_computation | async-start | bytes 3145728 | tf_op jit(solution)/shard_map/all_gather | solution.py:72
  7.9 73.1 %copy-start = (bf16[1,64,8192]{2,1,0:T(8,128)(2,1)S(1)}, bf16[1,64,8192]{2,1,0:T(8,128)(2,1)}, u32[]{:S(2)}) copy-start(bf16[1,64,8192]{2,1,0:T(8,128)(2,1)} %param.11) | copy-start | bytes 3145732
  7.9 72.1 %all-gather.6.cloned.1.call-start = ((), (), s32[]{:S(2)}) async-start(), calls=%async_computation.1 | async-start | bytes 3145728 | tf_op jit(solution)/shard_map/all_gather | solution.py:73
  8.7 570.9 %all-gather.8.cloned.1.call-start = ((), (), s32[]{:S(2)}) async-start(), calls=%async_computation.2 | async-start | bytes 35651584 | tf_op jit(solution)/shard_map/all_gather | solution.py:12
  83.5 8.2 %collective-permute-start = (bf16[16,8192]{1,0:T(8,128)(2,1)}, bf16[16,8192]{1,0:T(8,128)(2,1)S(1)}, u32[]{:S(2)}, u32[]{:S(2)}) collective-permute-start(bf16[16,8192]{1,0:T(8,128)(2,1)} %fusion.98), channel_id=1, source_target_pairs={{0,16},{1,17},{2,18},{3,19},{4,20},{5,21},{6,22},{7,23},{8,24},{9,... | collective-permute-start | bytes 786440 | tf_op jit(solution)/shard_map/while/body/eval_jaxpr/ppermute | solution.py:19
  95.0 9.4 %collective-permute-start = (bf16[16,8192]{1,0:T(8,128)(2,1)}, bf16[16,8192]{1,0:T(8,128)(2,1)S(1)}, u32[]{:S(2)}, u32[]{:S(2)}) collective-permute-start(bf16[16,8192]{1,0:T(8,128)(2,1)} %fusion.98), channel_id=1, source_target_pairs={{0,16},{1,17},{2,18},{3,19},{4,20},{5,21},{6,22},{7,23},{8,24},{9,... | collective-permute-start | bytes 786440 | tf_op jit(solution)/shard_map/while/body/eval_jaxpr/ppermute | solution.py:19
  107.5 8.5 %collective-permute-start = (bf16[16,8192]{1,0:T(8,128)(2,1)}, bf16[16,8192]{1,0:T(8,128)(2,1)S(1)}, u32[]{:S(2)}, u32[]{:S(2)}) collective-permute-start(bf16[16,8192]{1,0:T(8,128)(2,1)} %fusion.98), channel_id=1, source_target_pairs={{0,16},{1,17},{2,18},{3,19},{4,20},{5,21},{6,22},{7,23},{8,24},{9,... | collective-permute-start | bytes 786440 | tf_op jit(solution)/shard_map/while/body/eval_jaxpr/ppermute | solution.py:19
  119.3 8.5 %collective-permute-start = (bf16[16,8192]{1,0:T(8,128)(2,1)}, bf16[16,8192]{1,0:T(8,128)(2,1)S(1)}, u32[]{:S(2)}, u32[]{:S(2)}) collective-permute-start(bf16[16,8192]{1,0:T(8,128)(2,1)} %fusion.98), channel_id=1, source_target_pairs={{0,16},{1,17},{2,18},{3,19},{4,20},{5,21},{6,22},{7,23},{8,24},{9,... | collective-permute-start | bytes 786440 | tf_op jit(solution)/shard_map/while/body/eval_jaxpr/ppermute | solution.py:19
  131.0 8.5 %collective-permute-start = (bf16[16,8192]{1,0:T(8,128)(2,1)}, bf16[16,8192]{1,0:T(8,128)(2,1)S(1)}, u32[]{:S(2)}, u32[]{:S(2)}) collective-permute-start(bf16[16,8192]{1,0:T(8,128)(2,1)} %fusion.98), channel_id=1, source_target_pairs={{0,16},{1,17},{2,18},{3,19},{4,20},{5,21},{6,22},{7,23},{8,24},{9,... | collective-permute-start | bytes 786440 | tf_op jit(solution)/shard_map/while/body/eval_jaxpr/ppermute | solution.py:19
  142.8 8.5 %collective-permute-start = (bf16[16,8192]{1,0:T(8,128)(2,1)}, bf16[16,8192]{1,0:T(8,128)(2,1)S(1)}, u32[]{:S(2)}, u32[]{:S(2)}) collective-permute-start(bf16[16,8192]{1,0:T(8,128)(2,1)} %fusion.98), channel_id=1, source_target_pairs={{0,16},{1,17},{2,18},{3,19},{4,20},{5,21},{6,22},{7,23},{8,24},{9,... | collective-permute-start | bytes 786440 | tf_op jit(solution)/shard_map/while/body/eval_jaxpr/ppermute | solution.py:19
  154.5 8.5 %collective-permute-start = (bf16[16,8192]{1,0:T(8,128)(2,1)}, bf16[16,8192]{1,0:T(8,128)(2,1)S(1)}, u32[]{:S(2)}, u32[]{:S(2)}) collective-permute-start(bf16[16,8192]{1,0:T(8,128)(2,1)} %fusion.98), channel_id=1, source_target_pairs={{0,16},{1,17},{2,18},{3,19},{4,20},{5,21},{6,22},{7,23},{8,24},{9,... | collective-permute-start | bytes 786440 | tf_op jit(solution)/shard_map/while/body/eval_jaxpr/ppermute | solution.py:19
  166.2 9.3 %collective-permute-start = (bf16[16,8192]{1,0:T(8,128)(2,1)}, bf16[16,8192]{1,0:T(8,128)(2,1)S(1)}, u32[]{:S(2)}, u32[]{:S(2)}) collective-permute-start(bf16[16,8192]{1,0:T(8,128)(2,1)} %fusion.98), channel_id=1, source_target_pairs={{0,16},{1,17},{2,18},{3,19},{4,20},{5,21},{6,22},{7,23},{8,24},{9,... | collective-permute-start | bytes 786440 | tf_op jit(solution)/shard_map/while/body/eval_jaxpr/ppermute | solution.py:19
  178.8 8.5 %collective-permute-start = (bf16[16,8192]{1,0:T(8,128)(2,1)}, bf16[16,8192]{1,0:T(8,128)(2,1)S(1)}, u32[]{:S(2)}, u32[]{:S(2)}) collective-permute-start(bf16[16,8192]{1,0:T(8,128)(2,1)} %fusion.98), channel_id=1, source_target_pairs={{0,16},{1,17},{2,18},{3,19},{4,20},{5,21},{6,22},{7,23},{8,24},{9,... | collective-permute-start | bytes 786440 | tf_op jit(solution)/shard_map/while/body/eval_jaxpr/ppermute | solution.py:19
  195.7 9.1 %collective-permute-start.1 = (bf16[16,8192]{1,0:T(8,128)(2,1)S(1)}, bf16[16,8192]{1,0:T(8,128)(2,1)S(1)}, u32[]{:S(2)}, u32[]{:S(2)}) collective-permute-start(bf16[16,8192]{1,0:T(8,128)(2,1)S(1)} %fusion.103), channel_id=1, source_target_pairs={{16,0},{17,1},{18,2},{19,3},{20,4},{21,5},{22,6},{23,7},{24,8},{25... | collective-permute-start | bytes 786440 | tf_op jit(solution)/shard_map/while/body/eval_jaxpr/ppermute | solution.py:19
  210.2 10.2 %collective-permute-start.1 = (bf16[16,8192]{1,0:T(8,128)(2,1)S(1)}, bf16[16,8192]{1,0:T(8,128)(2,1)S(1)}, u32[]{:S(2)}, u32[]{:S(2)}) collective-permute-start(bf16[16,8192]{1,0:T(8,128)(2,1)S(1)} %fusion.103), channel_id=1, source_target_pairs={{16,0},{17,1},{18,2},{19,3},{20,4},{21,5},{22,6},{23,7},{24,8},{25... | collective-permute-start | bytes 786440 | tf_op jit(solution)/shard_map/while/body/eval_jaxpr/ppermute | solution.py:19
  225.9 10.8 %collective-permute-start.1 = (bf16[16,8192]{1,0:T(8,128)(2,1)S(1)}, bf16[16,8192]{1,0:T(8,128)(2,1)S(1)}, u32[]{:S(2)}, u32[]{:S(2)}) collective-permute-start(bf16[16,8192]{1,0:T(8,128)(2,1)S(1)} %fusion.103), channel_id=1, source_target_pairs={{16,0},{17,1},{18,2},{19,3},{20,4},{21,5},{22,6},{23,7},{24,8},{25... | collective-permute-start | bytes 786440 | tf_op jit(solution)/shard_map/while/body/eval_jaxpr/ppermute | solution.py:19
  242.2 9.9 %collective-permute-start.1 = (bf16[16,8192]{1,0:T(8,128)(2,1)S(1)}, bf16[16,8192]{1,0:T(8,128)(2,1)S(1)}, u32[]{:S(2)}, u32[]{:S(2)}) collective-permute-start(bf16[16,8192]{1,0:T(8,128)(2,1)S(1)} %fusion.103), channel_id=1, source_target_pairs={{16,0},{17,1},{18,2},{19,3},{20,4},{21,5},{22,6},{23,7},{24,8},{25... | collective-permute-start | bytes 786440 | tf_op jit(solution)/shard_map/while/body/eval_jaxpr/ppermute | solution.py:19
  257.6 9.1 %collective-permute-start.1 = (bf16[16,8192]{1,0:T(8,128)(2,1)S(1)}, bf16[16,8192]{1,0:T(8,128)(2,1)S(1)}, u32[]{:S(2)}, u32[]{:S(2)}) collective-permute-start(bf16[16,8192]{1,0:T(8,128)(2,1)S(1)} %fusion.103), channel_id=1, source_target_pairs={{16,0},{17,1},{18,2},{19,3},{20,4},{21,5},{22,6},{23,7},{24,8},{25... | collective-permute-start | bytes 786440 | tf_op jit(solution)/shard_map/while/body/eval_jaxpr/ppermute | solution.py:19
  272.1 8.3 %collective-permute-start.1 = (bf16[16,8192]{1,0:T(8,128)(2,1)S(1)}, bf16[16,8192]{1,0:T(8,128)(2,1)S(1)}, u32[]{:S(2)}, u32[]{:S(2)}) collective-permute-start(bf16[16,8192]{1,0:T(8,128)(2,1)S(1)} %fusion.103), channel_id=1, source_target_pairs={{16,0},{17,1},{18,2},{19,3},{20,4},{21,5},{22,6},{23,7},{24,8},{25... | collective-permute-start | bytes 786440 | tf_op jit(solution)/shard_map/while/body/eval_jaxpr/ppermute | solution.py:19
  285.8 8.3 %collective-permute-start.1 = (bf16[16,8192]{1,0:T(8,128)(2,1)S(1)}, bf16[16,8192]{1,0:T(8,128)(2,1)S(1)}, u32[]{:S(2)}, u32[]{:S(2)}) collective-permute-start(bf16[16,8192]{1,0:T(8,128)(2,1)S(1)} %fusion.103), channel_id=1, source_target_pairs={{16,0},{17,1},{18,2},{19,3},{20,4},{21,5},{22,6},{23,7},{24,8},{25... | collective-permute-start | bytes 786440 | tf_op jit(solution)/shard_map/while/body/eval_jaxpr/ppermute | solution.py:19
  299.5 8.3 %collective-permute-start.1 = (bf16[16,8192]{1,0:T(8,128)(2,1)S(1)}, bf16[16,8192]{1,0:T(8,128)(2,1)S(1)}, u32[]{:S(2)}, u32[]{:S(2)}) collective-permute-start(bf16[16,8192]{1,0:T(8,128)(2,1)S(1)} %fusion.103), channel_id=1, source_target_pairs={{16,0},{17,1},{18,2},{19,3},{20,4},{21,5},{22,6},{23,7},{24,8},{25... | collective-permute-start | bytes 786440 | tf_op jit(solution)/shard_map/while/body/eval_jaxpr/ppermute | solution.py:19
  313.2 8.3 %collective-permute-start.1 = (bf16[16,8192]{1,0:T(8,128)(2,1)S(1)}, bf16[16,8192]{1,0:T(8,128)(2,1)S(1)}, u32[]{:S(2)}, u32[]{:S(2)}) collective-permute-start(bf16[16,8192]{1,0:T(8,128)(2,1)S(1)} %fusion.103), channel_id=1, source_target_pairs={{16,0},{17,1},{18,2},{19,3},{20,4},{21,5},{22,6},{23,7},{24,8},{25... | collective-permute-start | bytes 786440 | tf_op jit(solution)/shard_map/while/body/eval_jaxpr/ppermute | solution.py:19
  329.3 4.2 copy-start.10
  411.6 4.9 copy-start.2
  (24 other events, 29.0 us)
Sparse Core Ops, SparseCore 0:
  9.5 35.8 all-gather.3
  46.9 33.0 all-gather.5
  411.7 167.8 all-gather.7
